TPU v7x, 256 devices: a whole 4x4x8 slice. The times are simulated.
256 devices in a mesh: lat: 8 (over x_lo, y), lon: 32 (over z, x_hi, core).
Axes of the slice: x: 4 (x_hi: 2, x_lo: 2; x = x_hi * 2 + x_lo), y: 4, z: 8, core: 2. Of those that a mesh axis runs over, the one named last changes fastest.
Arguments:
- activations: bfloat16 [4, 32, 2880, 512], P(None, 'lat', 'lon'), may hold values from -48 to 48
- upstream: bfloat16 [4, 32, 2880, 512], P(None, 'lat', 'lon'), may hold values from -6 to 6
- master: float32 [512, 9, 512], P(('lat', 'lon')), may hold values from -0.09375 to 0.09375
- moment_one: float32 [512, 9, 512], P(('lat', 'lon')), may hold values from -2.5 to 2.5
- moment_two: float32 [512, 9, 512], P(('lat', 'lon')), may hold values from 0.01 to 1
Outputs:
- input_grad: bfloat16 [4, 32, 2880, 512], P(None, 'lat', 'lon')
- new_weights: bfloat16 [512, 9, 512], replicated
- new_master: float32 [512, 9, 512], P(('lat', 'lon'))
- new_moment_one: float32 [512, 9, 512], P(('lat', 'lon'))
- new_moment_two: float32 [512, 9, 512], P(('lat', 'lon'))
- clipped_grad: float32 [512, 9, 512], P(('lat', 'lon'))
All inputs are finite; a program needn't handle non-finite values.
Results may differ from a plain program's by a relative error of at most 0.0049.
Values may be sent and summed in bfloat16 or wider, within the bound.
No kernel may reach another device: no remote copies, remote signals or barrier semaphores. Data moves between devices by JAX's collectives and lax.ppermute only.
A program may use at most 128 MiB of HBM per device.

v0:
```python
import functools
import math
import jax
import jax.numpy as jnp
from jax import lax
from jax.sharding import Mesh
from jax.sharding import PartitionSpec as P

CIN = 512
COUT = 512
TAPS = 9
LAT = ("lat_0", "lat_1")
LAT_LON = ("lat_0", "lat_1", "lon_0", "lon_1", "lon_2")
LON = ("lon_0", "lon_1", "lon_2")
learn_rate = 0.01
beta_one = 0.9
beta_two = 0.999
adam_eps = 1e-08
decay_rate = 0.1
step_count = 10.0
norm_eps = 1e-06


def padded(block, sides, width):
    for axis, dim in sides:
        count = lax.axis_size(axis)
        forward = [(i, i + 1) for i in range(count - 1)]
        forward.append((count - 1, 0))
        backward = [(target, source) for source, target in forward]
        low = lax.ppermute(
            lax.slice_in_dim(block, block.shape[dim] - width, None, axis=dim), axis, forward
        )
        high = lax.ppermute(lax.slice_in_dim(block, 0, width, axis=dim), axis, backward)
        block = jnp.concatenate([low, block, high], axis=dim)
    return block


def sent_to_all(shard, axis):
    copies = jnp.broadcast_to(shard, (lax.axis_size(axis), *shard.shape))
    return lax.all_to_all(copies, axis, split_axis=0, concat_axis=0, tiled=True)


def joined_along(parts, dim):
    shape = list(parts.shape[1:])
    shape[dim] *= parts.shape[0]
    return jnp.moveaxis(parts, 0, dim).reshape(shape)


def gathered_copies(shard, axis, dim):
    parts = sent_to_all(shard, axis)
    return joined_along(parts, dim)


def split_up(shard, dim, count):
    before, after = (shard.shape[:dim], shard.shape[dim + 1 :])
    return jnp.moveaxis(shard.reshape(*before, count, -1, *after), dim, 0)


def sent_and_summed(shard, axis, dim):
    count = lax.axis_size(axis)
    parts = lax.all_to_all(split_up(shard, dim, count), axis, 0, 0, tiled=True)
    return jnp.sum(parts, axis=0)


def by_axis(shard, axes):
    return functools.reduce(lax.psum, axes, shard)


def mask_poles(wide_field):
    lat_index = lax.axis_index(LAT)
    lat_count = lax.axis_size(LAT)
    total_rows = wide_field.shape[1]
    row_ids = lax.broadcasted_iota(jnp.int32, (1, total_rows, 1, 1), 1)
    upper = jnp.logical_and(row_ids == 0, lat_index == 0)
    lower = jnp.logical_and(row_ids == total_rows - 1, lat_index == lat_count - 1)
    return jnp.where(jnp.logical_or(upper, lower), jnp.zeros((), wide_field.dtype), wide_field)


def pull_product(grad_wide, lat_rows, lon_cols):
    batch_rows = grad_wide.shape[0]
    out_width = grad_wide.shape[3]
    windows = []
    for tap_index in range(9):
        row_off, col_off = divmod(tap_index, 3)
        windows.append(
            grad_wide[
                :, 2 - row_off : 2 - row_off + lat_rows, 2 - col_off : 2 - col_off + lon_cols, :
            ].reshape(-1, out_width)
        )

    def pull_compute(shard_piece, first_row):
        piece_width = shard_piece.shape[0]
        summed = jnp.zeros((batch_rows * lat_rows * lon_cols, piece_width), jnp.float32)
        for tap_index in range(9):
            summed = summed + lax.dot_general(
                windows[tap_index],
                shard_piece[:, tap_index, :],
                (((1,), (1,)), ((), ())),
                preferred_element_type=jnp.float32,
            )
        return summed.reshape(batch_rows, lat_rows, lon_cols, piece_width)

    return pull_compute


def input_taps(act_wide, grad_flat, lat_rows, lon_cols):

    def input_compute(first_row, row_count):
        tap_parts = []
        for tap_index in range(9):
            row_off, col_off = divmod(tap_index, 3)
            tap_slab = act_wide[
                :, row_off : row_off + lat_rows, col_off : col_off + lon_cols, :
            ].reshape(-1, row_count)
            tap_parts.append(
                lax.dot_general(
                    tap_slab,
                    grad_flat,
                    (((0,), (0,)), ((), ())),
                    preferred_element_type=jnp.float32,
                )
            )
        return jnp.stack(tap_parts, axis=1)

    return input_compute


def per_device(activations, upstream, master, moment_one, moment_two):
    lat_rows = activations.shape[1]
    lon_cols = activations.shape[2]
    grad_flat = upstream.reshape(-1, upstream.shape[3])
    act_wide = mask_poles(padded(activations, ((LAT, 1), (LON, 2)), 1))
    grad_wide = mask_poles(padded(upstream, ((LAT, 1), (LON, 2)), 1))
    producer = pull_product(grad_wide, lat_rows, lon_cols)
    term_maker = input_taps(act_wide, grad_flat, lat_rows, lon_cols)
    old_weights = master.astype(jnp.bfloat16)
    old_block = gathered_copies(old_weights, LON, 0)
    data_sum = producer(lax.all_gather(old_block, LAT, axis=0, tiled=True), jnp.int32(0))
    input_grad = data_sum.astype(jnp.bfloat16)
    shard_rows = master.shape[0]
    lat_block = lax.psum_scatter(
        term_maker(jnp.int32(0), lax.axis_size(LAT) * (shard_rows * lax.axis_size(LON))),
        LAT,
        scatter_dimension=0,
        tiled=True,
    )
    grad_shard = sent_and_summed(lat_block, LON, 0)
    max_norm = math.sqrt(float(CIN * TAPS * COUT))
    square_sum = by_axis(jnp.sum(grad_shard * grad_shard), LAT_LON)
    clip_factor = jnp.minimum(1.0, max_norm / (jnp.sqrt(square_sum) + norm_eps))
    grad_scaled = clip_factor * grad_shard
    new_one = beta_one * moment_one + (1.0 - beta_one) * grad_scaled
    new_two = beta_two * moment_two + (1.0 - beta_two) * grad_scaled * grad_scaled
    first_hat = new_one / (1.0 - beta_one**step_count)
    second_hat = new_two / (1.0 - beta_two**step_count)
    new_master = master - learn_rate * (
        first_hat / (jnp.sqrt(second_hat) + adam_eps) + decay_rate * master
    )
    new_half = new_master.astype(jnp.bfloat16)
    lon_block = gathered_copies(new_half, LON, 0)
    new_weights = lax.all_gather(lon_block, LAT, axis=0, tiled=True)
    return (input_grad, new_weights, new_master, new_one, new_two, grad_scaled)


def solution(mesh):
    split = Mesh(mesh.devices.reshape(2, 4, 8, 2, 2), ("lat_0", "lat_1", "lon_0", "lon_1", "lon_2"))
    in_specs = (
        P(None, LAT, LON, None),
        P(None, LAT, LON, None),
        P(LAT_LON, None, None),
        P(LAT_LON, None, None),
        P(LAT_LON, None, None),
    )
    out_specs = (
        P(None, LAT, LON, None),
        P(),
        P(LAT_LON, None, None),
        P(LAT_LON, None, None),
        P(LAT_LON, None, None),
        P(LAT_LON, None, None),
    )
    return jax.shard_map(
        per_device, mesh=split, in_specs=in_specs, out_specs=out_specs, check_vma=False
    )
```

profile of v0, /device:TPU:1, one launch (start us, length us, event | category | flops | bytes accessed | tf_op | source)
XLA Modules:
  0.0 432.9 jit_solution(12576936133788156169)
XLA Ops:
  7.2 3.2 fusion.90
  11.2 2.1 collective-permute-start
  14.2 2.4 collective-permute-start.1
  18.4 3.6 collective-permute-start.5
  25.4 6.9 %collective-permute-start.2 = (bf16[4,6,1,512]{3,2,1,0:T(2,128)(2,1)S(1)}, bf16[4,6,1,512]{3,2,1,0:T(2,128)(2,1)S(1)}, u32[]{:S(2)}, u32[]{:S(2)}) collective-permute-start(bf16[4,6,1,512]{3,2,1,0:T(2,128)(2,1)S(1)} %get-tuple-element.46), channel_id=1, source_target_pairs={{0,1},{1,2},{2,3},{3,4},{4,5},{5,6},{6,7},{7,8},{8,9},{9,10},{10,1... | collective-permute-start | bytes 73736 | tf_op jit(solution)/shard_map/ppermute | solution.py:30
  34.8 4.8 %collective-permute-start.6 = (bf16[4,6,1,512]{3,2,1,0:T(2,128)(2,1)S(1)}, bf16[4,6,1,512]{3,2,1,0:T(2,128)(2,1)S(1)}, u32[]{:S(2)}, u32[]{:S(2)}) collective-permute-start(bf16[4,6,1,512]{3,2,1,0:T(2,128)(2,1)S(1)} %get-tuple-element.35), channel_id=1, source_target_pairs={{0,1},{1,2},{2,3},{3,4},{4,5},{5,6},{6,7},{7,8},{8,9},{9,10},{10,1... | collective-permute-start | bytes 73736 | tf_op jit(solution)/shard_map/ppermute | solution.py:30
  39.6 10.4 %collective-permute-start.7 = (bf16[4,6,1,512]{3,2,1,0:T(2,128)(2,1)S(1)}, bf16[4,6,1,512]{3,2,1,0:T(2,128)(2,1)S(1)}, u32[]{:S(2)}, u32[]{:S(2)}) collective-permute-start(bf16[4,6,1,512]{3,2,1,0:T(2,128)(2,1)S(1)} %get-tuple-element.36), channel_id=1, source_target_pairs={{1,0},{2,1},{3,2},{4,3},{5,4},{6,5},{7,6},{8,7},{9,8},{10,9},{11,1... | collective-permute-start | bytes 73736 | tf_op jit(solution)/shard_map/ppermute | solution.py:33
  50.1 4.9 %collective-permute-done.7 = bf16[4,6,1,512]{3,2,1,0:T(2,128)(2,1)S(1)} collective-permute-done((bf16[4,6,1,512]{3,2,1,0:T(2,128)(2,1)S(1)}, bf16[4,6,1,512]{3,2,1,0:T(2,128)(2,1)S(1)}, u32[]{:S(2)}, u32[]{:S(2)}) %collective-permute-start.7) | collective-permute-done | bytes 24608 | tf_op jit(solution)/shard_map/ppermute | solution.py:33
  55.0 2.7 maximum_select_fusion.1
  67.8 2.0 fusion.52
  71.8 2.1 fusion.64
  73.9 2.1 fusion.70
  76.0 108.3 %reduce-scatter.2.cloned.1.call-done = f32[64,9,512]{2,0,1:T(8,128)} async-done(((f32[512,9,512]{2,0,1:T(8,128)}), f32[64,9,512]{2,0,1:T(8,128)}) %reduce-scatter.2.cloned.1.call-update) | async-done | bytes 1179664 | tf_op jit(solution)/shard_map/reduce_scatter | solution.py:141
  186.8 42.6 %all_to_all.15 = f32[32,2,9,512]{3,1,2,0:T(2,128)S(1)} all-to-all(f32[32,2,9,512]{3,1,2,0:T(2,128)S(1)} %copy.78), channel_id=1, replica_groups=mesh['lat_0'=2,'lat_1'=4,'lon_0'=8,'lon_1'=2,'lon_2'=2] {'lon_0','lon_1'..., dimensions={0} | all-to-all | bytes 2359296 | tf_op jit(solution)/shard_map/all_to_all | solution.py:61
  231.7 4.4 %psum.35 = f32[]{:T(128)} all-reduce(f32[]{:T(128)} %multiply_reduce_fusion), channel_id=1, replica_groups=mesh['lat_0'=2,'lat_1'=4,'lon_0'=8,'lon_1'=2,'lon_2'=2] {'lat_0'}, use_global_device_ids=true, to_apply=%region_3.4 | all-reduce | flops 1 | bytes 8 | tf_op jit(solution)/shard_map/psum | solution.py:66
  236.1 6.8 %psum.36 = f32[]{:T(128)} all-reduce(f32[]{:T(128)} %psum.35), channel_id=1, replica_groups=mesh['lat_0'=2,'lat_1'=4,'lon_0'=8,'lon_1'=2,'lon_2'=2] {'lat_1'}, use_global_device_ids=true, to_apply=%region_4.5 | all-reduce | flops 1 | bytes 8 | tf_op jit(solution)/shard_map/psum | solution.py:66
  242.9 12.3 %psum.37 = f32[]{:T(128)} all-reduce(f32[]{:T(128)} %psum.36), channel_id=1, replica_groups=mesh['lat_0'=2,'lat_1'=4,'lon_0'=8,'lon_1'=2,'lon_2'=2] {'lon_0'}, use_global_device_ids=true, to_apply=%region_5.6 | all-reduce | flops 1 | bytes 8 | tf_op jit(solution)/shard_map/psum | solution.py:66
  255.3 5.9 %psum.38 = f32[]{:T(128)} all-reduce(f32[]{:T(128)} %psum.37), channel_id=1, replica_groups=mesh['lat_0'=2,'lat_1'=4,'lon_0'=8,'lon_1'=2,'lon_2'=2] {'lon_1'}, use_global_device_ids=true, to_apply=%region_6.7 | all-reduce | flops 1 | bytes 8 | tf_op jit(solution)/shard_map/psum | solution.py:66
  261.2 11.5 %psum.39 = f32[]{:T(128)} all-reduce(f32[]{:T(128)} %psum.38), channel_id=1, replica_groups=mesh['lat_0'=2,'lat_1'=4,'lon_0'=8,'lon_1'=2,'lon_2'=2] {'lon_2'}, use_global_device_ids=true, to_apply=%region_7.8 | all-reduce | flops 1 | bytes 8 | tf_op jit(solution)/shard_map/psum | solution.py:66
  275.4 23.0 %all_to_all.16 = bf16[32,2,9,512]{3,1,2,0:T(2,128)(2,1)S(1)} all-to-all(bf16[32,2,9,512]{3,1,2,0:T(2,128)(2,1)S(1)} %broadcast_in_dim.24), channel_id=1, replica_groups=mesh['lat_0'=2,'lat_1'=4,'lon_0'=8,'lon_1'=2,'lon_2'=2] {'lon_0','lon_1'..., dimensions={0} | all-to-all | bytes 1179648 | tf_op jit(solution)/shard_map/all_to_all | solution.py:40
  300.4 23.7 %all_to_all.17 = bf16[32,2,9,512]{3,1,2,0:T(2,128)(2,1)S(1)} all-to-all(bf16[32,2,9,512]{3,1,2,0:T(2,128)(2,1)S(1)} %broadcast_in_dim.25), channel_id=1, replica_groups=mesh['lat_0'=2,'lat_1'=4,'lon_0'=8,'lon_1'=2,'lon_2'=2] {'lon_0','lon_1'..., dimensions={0} | all-to-all | bytes 1179648 | tf_op jit(solution)/shard_map/all_to_all | solution.py:40
  325.7 6.2 %fusion.87 = (bf16[4,4,90,512]{3,2,1,0:T(8,128)(2,1)}, bf16[4,4,90,512]{3,2,1,0:T(8,128)(2,1)}, bf16[4,4,90,512]{3,2,1,0:T(8,128)(2,1)}, bf16[4,4,90,512]{3,2,1,...) fusion(bf16[4,6,92,512]{3,2,1,0:T(8,128)(2,1)S(1)} %get-tuple-e, ...), kind=kLoop, calls=%fused_computation.81 | loop fusion | bytes 26542080 | tf_op jit(solution)/shard_map/slice | solution.py:86
  333.6 2.5 reshape.77
  337.4 2.6 reshape.79
  340.0 2.5 reshape.80
  343.8 2.6 reshape.82
  346.4 2.5 reshape.83
  350.2 10.2 %all-gather.3.cloned.1.call-done = bf16[512,9,512]{2,0,1:T(8,128)(2,1)} async-done(((bf16[64,9,512]{2,0,1:T(8,128)(2,1)}), bf16[512,9,512]{2,0,1:T(8,128)(2,1)}) %all-gather.3.cloned.1.call-update) | async-done | bytes 4718608 | tf_op jit(solution)/shard_map/all_gather | solution.py:138
  360.4 2.2 fusion.73
  374.0 2.3 copy.80
  376.2 45.0 %all-gather.5.cloned.1.call-done = bf16[512,9,512]{2,0,1:T(8,128)(2,1)} async-done(((bf16[64,9,512]{2,0,1:T(8,128)(2,1)}), bf16[512,9,512]{2,0,1:T(8,128)(2,1)}) %all-gather.5.cloned.1.call-update) | async-done | bytes 4718608 | tf_op jit(solution)/shard_map/all_gather | solution.py:161
  421.2 4.8 %copy.127 = bf16[512,9,512]{2,0,1:T(8,128)(2,1)} copy(bf16[512,9,512]{2,0,1:T(8,128)(2,1)} %all-gather.5.cloned.1.call-done) | data formatting | bytes 9437184
  (89 shorter events, 48.7 us)
Async XLA Ops:
  7.2 9.4 %copy-start.3 = (bf16[4,4,90,512]{3,1,2,0:T(4,128)(2,1)S(1)}, bf16[4,4,90,512]{3,1,2,0:T(4,128)(2,1)}, u32[]{:S(2)}) copy-start(bf16[4,4,90,512]{3,1,2,0:T(4,128)(2,1)} %param.5) | copy-start | bytes 4423684
  7.2 177.2 %reduce-scatter.2.cloned.1.call-start = ((), (), s32[]{:S(2)}) async-start(), calls=%async_computation.5 | async-start | bytes 10616832 | tf_op jit(solution)/shard_map/reduce_scatter | solution.py:141
  11.2 11.7 %collective-permute-start = (bf16[4,1,90,512]{3,2,1,0:T(8,128)(2,1)}, bf16[4,1,90,512]{3,2,1,0:T(8,128)(2,1)}, u32[]{:S(2)}, u32[]{:S(2)}) collective-permute-start(bf16[4,1,90,512]{3,2,1,0:T(8,128)(2,1)} %copy.110), channel_id=1, source_target_pairs={{0,32},{32,64},{64,96},{96,128},{128,160},{160,192},{192,224},{224... | collective-permute-start | bytes 1105928 | tf_op jit(solution)/shard_map/ppermute | solution.py:30
  14.2 9.8 %copy-start.4 = (bf16[4,4,90,512]{3,1,2,0:T(4,128)(2,1)S(1)}, bf16[4,4,90,512]{3,1,2,0:T(4,128)(2,1)}, u32[]{:S(2)}) copy-start(bf16[4,4,90,512]{3,1,2,0:T(4,128)(2,1)} %param.6) | copy-start | bytes 4423684
  14.2 10.1 %collective-permute-start.1 = (bf16[4,1,90,512]{3,2,1,0:T(8,128)(2,1)}, bf16[4,1,90,512]{3,2,1,0:T(8,128)(2,1)}, u32[]{:S(2)}, u32[]{:S(2)}) collective-permute-start(bf16[4,1,90,512]{3,2,1,0:T(8,128)(2,1)} %copy.111), channel_id=1, source_target_pairs={{32,0},{64,32},{96,64},{128,96},{160,128},{192,160},{224,192},{0,2... | collective-permute-start | bytes 1105928 | tf_op jit(solution)/shard_map/ppermute | solution.py:33
  18.4 14.0 %collective-permute-start.4 = (bf16[4,1,90,512]{3,2,1,0:T(8,128)(2,1)}, bf16[4,1,90,512]{3,2,1,0:T(8,128)(2,1)}, u32[]{:S(2)}, u32[]{:S(2)}) collective-permute-start(bf16[4,1,90,512]{3,2,1,0:T(8,128)(2,1)} %copy.112), channel_id=1, source_target_pairs={{0,32},{32,64},{64,96},{96,128},{128,160},{160,192},{192,224},{224... | collective-permute-start | bytes 1105928 | tf_op jit(solution)/shard_map/ppermute | solution.py:30
  18.4 15.3 %collective-permute-start.5 = (bf16[4,1,90,512]{3,2,1,0:T(8,128)(2,1)S(1)}, bf16[4,1,90,512]{3,2,1,0:T(8,128)(2,1)}, u32[]{:S(2)}, u32[]{:S(2)}) collective-permute-start(bf16[4,1,90,512]{3,2,1,0:T(8,128)(2,1)S(1)} %copy.113), channel_id=1, source_target_pairs={{32,0},{64,32},{96,64},{128,96},{160,128},{192,160},{224,192},{0,2... | collective-permute-start | bytes 1105928 | tf_op jit(solution)/shard_map/ppermute | solution.py:33
  25.4 24.6 %collective-permute-start.2 = (bf16[4,6,1,512]{3,2,1,0:T(2,128)(2,1)S(1)}, bf16[4,6,1,512]{3,2,1,0:T(2,128)(2,1)S(1)}, u32[]{:S(2)}, u32[]{:S(2)}) collective-permute-start(bf16[4,6,1,512]{3,2,1,0:T(2,128)(2,1)S(1)} %get-tuple-element.46), channel_id=1, source_target_pairs={{0,1},{1,2},{2,3},{3,4},{4,5},{5,6},{6,7},{7,8},{8,9},{9,10},{10,1... | collective-permute-start | bytes 73736 | tf_op jit(solution)/shard_map/ppermute | solution.py:30
  32.3 17.7 %collective-permute-start.3 = (bf16[4,6,1,512]{3,2,1,0:T(2,128)(2,1)S(1)}, bf16[4,6,1,512]{3,2,1,0:T(2,128)(2,1)S(1)}, u32[]{:S(2)}, u32[]{:S(2)}) collective-permute-start(bf16[4,6,1,512]{3,2,1,0:T(2,128)(2,1)S(1)} %get-tuple-element.47), channel_id=1, source_target_pairs={{1,0},{2,1},{3,2},{4,3},{5,4},{6,5},{7,6},{8,7},{9,8},{10,9},{11,1... | collective-permute-start | bytes 73736 | tf_op jit(solution)/shard_map/ppermute | solution.py:33
  34.8 15.2 %collective-permute-start.6 = (bf16[4,6,1,512]{3,2,1,0:T(2,128)(2,1)S(1)}, bf16[4,6,1,512]{3,2,1,0:T(2,128)(2,1)S(1)}, u32[]{:S(2)}, u32[]{:S(2)}) collective-permute-start(bf16[4,6,1,512]{3,2,1,0:T(2,128)(2,1)S(1)} %get-tuple-element.35), channel_id=1, source_target_pairs={{0,1},{1,2},{2,3},{3,4},{4,5},{5,6},{6,7},{7,8},{8,9},{9,10},{10,1... | collective-permute-start | bytes 73736 | tf_op jit(solution)/shard_map/ppermute | solution.py:30
  39.6 15.4 %collective-permute-start.7 = (bf16[4,6,1,512]{3,2,1,0:T(2,128)(2,1)S(1)}, bf16[4,6,1,512]{3,2,1,0:T(2,128)(2,1)S(1)}, u32[]{:S(2)}, u32[]{:S(2)}) collective-permute-start(bf16[4,6,1,512]{3,2,1,0:T(2,128)(2,1)S(1)} %get-tuple-element.36), channel_id=1, source_target_pairs={{1,0},{2,1},{3,2},{4,3},{5,4},{6,5},{7,6},{8,7},{9,8},{10,9},{11,1... | collective-permute-start | bytes 73736 | tf_op jit(solution)/shard_map/ppermute | solution.py:33
  50.0 7.7 %copy-start.5 = (bf16[4,4,90,512]{3,1,2,0:T(4,128)(2,1)S(1)}, bf16[4,4,90,512]{3,1,2,0:T(4,128)(2,1)}, u32[]{:S(2)}) copy-start(bf16[4,4,90,512]{3,1,2,0:T(4,128)(2,1)} %param.6) | copy-start | bytes 4423684
  76.0 284.4 %all-gather.3.cloned.1.call-start = ((), (), s32[]{:S(2)}) async-start(), calls=%async_computation.4 | async-start | bytes 5308416 | tf_op jit(solution)/shard_map/all_gather | solution.py:138
  300.0 121.2 %all-gather.5.cloned.1.call-start = ((), (), s32[]{:S(2)}) async-start(), calls=%async_computation.6 | async-start | bytes 5308416 | tf_op jit(solution)/shard_map/all_gather | solution.py:161
  331.9 4.2 copy-start.2
  337.4 5.1 %copy-start.1 = (bf16[4,4,90,512]{3,2,1,0:T(8,128)(2,1)S(1)}, bf16[4,4,90,512]{3,2,1,0:T(8,128)(2,1)}, u32[]{:S(2)}) copy-start(bf16[4,4,90,512]{3,2,1,0:T(8,128)(2,1)} %get-tuple-element.40) | copy-start | bytes 4423684
  343.8 5.1 %copy-start = (bf16[4,4,90,512]{3,2,1,0:T(8,128)(2,1)S(1)}, bf16[4,4,90,512]{3,2,1,0:T(8,128)(2,1)}, u32[]{:S(2)}) copy-start(bf16[4,4,90,512]{3,2,1,0:T(8,128)(2,1)} %get-tuple-element.37) | copy-start | bytes 4423684
  350.2 12.4 %copy-start.13 = (bf16[1440,512]{1,0:T(8,128)(2,1)S(1)}, bf16[1440,512]{1,0:T(8,128)(2,1)}, u32[]{:S(2)}) copy-start(bf16[1440,512]{1,0:T(8,128)(2,1)} %reshape.77) | copy-start | bytes 4423684
  360.4 2.5 copy-start.14
  362.9 1.4 copy-start.12
  364.3 1.4 copy-start.11
  365.7 1.4 copy-start.10
  367.0 1.4 copy-start.9
  368.4 1.4 copy-start.8
  369.8 1.4 copy-start.7
  371.1 1.4 copy-start.6
Sparse Core Ops, SparseCore 0:
  76.1 108.1 reduce-scatter.1
  300.1 60.2 all-gather.2
  362.2 58.9 all-gather.4
where the time goes:
time: 441 us; the launch traced here: 433 us
  waiting for transfers between devices  169 us (38%)
  blocking collectives  130 us (29%)
  local copies, waits for them, and re-layouts  52.8 us (12%)
  starting transfers between devices  30.3 us (7%)
  matrix products  28.2 us (6%)
  between operations  15.2 us (3%)
  other arithmetic  6.7 us (2%)
    reduce_scatter x1, waiting for transfers between devices, per_device(): lax.psum_scatter(term_maker(jnp.int32(0), lax.axis_size(LAT) * (shard_row...  108 us
    all_to_all x2, blocking collectives, sent_to_all(): return lax.all_to_all(copies, axis, split_axis=0, concat_axis=0, tiled=True)  46.8 us
    all_gather x1, waiting for transfers between devices, per_device(): new_weights = lax.all_gather(lon_block, LAT, axis=0, tiled=True)  45 us
    all_to_all x1, blocking collectives, sent_and_summed(): parts = lax.all_to_all(split_up(shard, dim, count), axis, 0, 0, tiled=True)  42.6 us
    psum x5, blocking collectives, by_axis(): return functools.reduce(lax.psum, axes, shard)  41 us
    reshape x9, local copies, waits for them, and re-layouts, pull_product(): windows.append(grad_wide[:, 2 - row_off:2 - row_off + lat_rows, 2 - col_o...  18.3 us
    dot_general x9, matrix products, input_compute(): lax.dot_general(tap_slab, grad_flat, (((0,), (0,)), ((), ())), preferred_...  18.3 us
    ppermute x4, starting transfers between devices, padded(): lax.ppermute(lax.slice_in_dim(block, 0, width, axis=dim), axis, backward)  16.4 us
  transfers between devices with their start and end apart: 11, of which 5 were waited for; matrix products, arithmetic and copies ran while one was open for 11% of the time, Pallas kernels for 0%

commit v1 on v0

--- a/solution.py
+++ b/solution.py
@@ -158,7 +158,9 @@
     )
     new_half = new_master.astype(jnp.bfloat16)
     lon_block = gathered_copies(new_half, LON, 0)
-    new_weights = lax.all_gather(lon_block, LAT, axis=0, tiled=True)
+    new_weights = jnp.concatenate(
+        lax.all_to_all(jnp.stack([lon_block] * lax.axis_size(LAT)), LAT, 0, 0), axis=0
+    )
     return (input_grad, new_weights, new_master, new_one, new_two, grad_scaled)
 
 

time: 441 us -> 458 us (1.039)
  waiting for transfers between devices: 169 us -> 178 us
  starting transfers between devices: 30.3 us -> 35.8 us
    all_to_all x0 -> x1, waiting for transfers between devices: none -> 64.2 us  [per_device(): lax.all_to_all(jnp.stack([lon_block] * lax.axis_size(LAT)), LAT, 0, 0)]
    all_gather x1 -> x0, waiting for transfers between devices: 45 us -> none  [per_device(): new_weights = lax.all_gather(lon_block, LAT, axis=0, tiled=True)]
    all_gather x1, waiting for transfers between devices: 10.2 us -> 0.01 us  [per_device(): lax.all_gather(old_block, LAT, axis=0, tiled=True)]
    all_to_all x0 -> x1, local copies, waits for them, and re-layouts: none -> 5.1 us  [per_device(): lax.all_to_all(jnp.stack([lon_block] * lax.axis_size(LAT)), LAT, 0, 0)]
    all_to_all x0 -> x1, starting transfers between devices: none -> 4.79 us  [per_device(): lax.all_to_all(jnp.stack([lon_block] * lax.axis_size(LAT)), LAT, 0, 0)]
    unnamed x40 -> x39, local copies, waits for them, and re-layouts: 15.4 us -> 11 us
  transfers between devices with their start and end apart: 11 -> 11, of which waited for: 5 -> 4; matrix products, arithmetic and copies ran while one was open for 11% -> 9% of each run, Pallas kernels for 0% -> 0%
where the time goes in v1:
time: 458 us; the launch traced here: 450 us
  waiting for transfers between devices  178 us (39%)
  blocking collectives  130 us (28%)
  local copies, waits for them, and re-layouts  55.4 us (12%)
  starting transfers between devices  35.8 us (8%)
  matrix products  28.2 us (6%)
  between operations  15.5 us (3%)
  other arithmetic  6.7 us (1%)
    reduce_scatter x1, waiting for transfers between devices, per_device(): lax.psum_scatter(term_maker(jnp.int32(0), lax.axis_size(LAT) * (shard_row...  108 us
    all_to_all x1, waiting for transfers between devices, per_device(): lax.all_to_all(jnp.stack([lon_block] * lax.axis_size(LAT)), LAT, 0, 0)  64.2 us
    all_to_all x2, blocking collectives, sent_to_all(): return lax.all_to_all(copies, axis, split_axis=0, concat_axis=0, tiled=True)  46.9 us
    all_to_all x1, blocking collectives, sent_and_summed(): parts = lax.all_to_all(split_up(shard, dim, count), axis, 0, 0, tiled=True)  42.6 us
    psum x5, blocking collectives, by_axis(): return functools.reduce(lax.psum, axes, shard)  41 us
    dot_general x9, matrix products, input_compute(): lax.dot_general(tap_slab, grad_flat, (((0,), (0,)), ((), ())), preferred_...  18.3 us
    reshape x9, local copies, waits for them, and re-layouts, pull_product(): windows.append(grad_wide[:, 2 - row_off:2 - row_off + lat_rows, 2 - col_o...  18.2 us
    ppermute x4, starting transfers between devices, padded(): lax.ppermute(lax.slice_in_dim(block, 0, width, axis=dim), axis, backward)  17.1 us
  transfers between devices with their start and end apart: 11, of which 4 were waited for; matrix products, arithmetic and copies ran while one was open for 9% of the time, Pallas kernels for 0%

profile of v1, /device:TPU:1, one launch (start us, length us, event | category | flops | bytes accessed | tf_op | source)
XLA Modules:
  0.0 450.4 jit_solution(6670414009180385931)
XLA Ops:
  7.2 3.2 fusion.90
  11.2 2.1 collective-permute-start
  14.2 2.4 collective-permute-start.1
  18.4 3.6 collective-permute-start.5
  25.4 6.9 %collective-permute-start.2 = (bf16[4,6,1,512]{3,2,1,0:T(2,128)(2,1)S(1)}, bf16[4,6,1,512]{3,2,1,0:T(2,128)(2,1)S(1)}, u32[]{:S(2)}, u32[]{:S(2)}) collective-permute-start(bf16[4,6,1,512]{3,2,1,0:T(2,128)(2,1)S(1)} %get-tuple-element.46), channel_id=1, source_target_pairs={{0,1},{1,2},{2,3},{3,4},{4,5},{5,6},{6,7},{7,8},{8,9},{9,10},{10,1... | collective-permute-start | bytes 73736 | tf_op jit(solution)/shard_map/ppermute | solution.py:30
  34.8 4.8 %collective-permute-start.6 = (bf16[4,6,1,512]{3,2,1,0:T(2,128)(2,1)S(1)}, bf16[4,6,1,512]{3,2,1,0:T(2,128)(2,1)S(1)}, u32[]{:S(2)}, u32[]{:S(2)}) collective-permute-start(bf16[4,6,1,512]{3,2,1,0:T(2,128)(2,1)S(1)} %get-tuple-element.35), channel_id=1, source_target_pairs={{0,1},{1,2},{2,3},{3,4},{4,5},{5,6},{6,7},{7,8},{8,9},{9,10},{10,1... | collective-permute-start | bytes 73736 | tf_op jit(solution)/shard_map/ppermute | solution.py:30
  39.6 11.1 %collective-permute-start.7 = (bf16[4,6,1,512]{3,2,1,0:T(2,128)(2,1)S(1)}, bf16[4,6,1,512]{3,2,1,0:T(2,128)(2,1)S(1)}, u32[]{:S(2)}, u32[]{:S(2)}) collective-permute-start(bf16[4,6,1,512]{3,2,1,0:T(2,128)(2,1)S(1)} %get-tuple-element.36), channel_id=1, source_target_pairs={{1,0},{2,1},{3,2},{4,3},{5,4},{6,5},{7,6},{8,7},{9,8},{10,9},{11,1... | collective-permute-start | bytes 73736 | tf_op jit(solution)/shard_map/ppermute | solution.py:33
  50.8 4.9 %collective-permute-done.7 = bf16[4,6,1,512]{3,2,1,0:T(2,128)(2,1)S(1)} collective-permute-done((bf16[4,6,1,512]{3,2,1,0:T(2,128)(2,1)S(1)}, bf16[4,6,1,512]{3,2,1,0:T(2,128)(2,1)S(1)}, u32[]{:S(2)}, u32[]{:S(2)}) %collective-permute-start.7) | collective-permute-done | bytes 24608 | tf_op jit(solution)/shard_map/ppermute | solution.py:33
  55.8 2.7 maximum_select_fusion.1
  72.6 2.1 fusion.64
  74.6 2.1 fusion.70
  76.8 108.3 %reduce-scatter.2.cloned.1.call-done = f32[64,9,512]{2,0,1:T(8,128)} async-done(((f32[512,9,512]{2,0,1:T(8,128)}), f32[64,9,512]{2,0,1:T(8,128)}) %reduce-scatter.2.cloned.1.call-update) | async-done | bytes 1179664 | tf_op jit(solution)/shard_map/reduce_scatter | solution.py:141
  187.5 42.6 %all_to_all.20 = f32[32,2,9,512]{3,1,2,0:T(2,128)S(1)} all-to-all(f32[32,2,9,512]{3,1,2,0:T(2,128)S(1)} %copy.78), channel_id=1, replica_groups=mesh['lat_0'=2,'lat_1'=4,'lon_0'=8,'lon_1'=2,'lon_2'=2] {'lon_0','lon_1'..., dimensions={0} | all-to-all | bytes 2359296 | tf_op jit(solution)/shard_map/all_to_all | solution.py:61
  232.5 4.4 psum.35
  236.9 6.8 %psum.36 = f32[]{:T(128)} all-reduce(f32[]{:T(128)} %psum.35), channel_id=1, replica_groups=mesh['lat_0'=2,'lat_1'=4,'lon_0'=8,'lon_1'=2,'lon_2'=2] {'lat_1'}, use_global_device_ids=true, to_apply=%region_4.5 | all-reduce | flops 1 | bytes 8 | tf_op jit(solution)/shard_map/psum | solution.py:66
  243.7 12.3 %psum.37 = f32[]{:T(128)} all-reduce(f32[]{:T(128)} %psum.36), channel_id=1, replica_groups=mesh['lat_0'=2,'lat_1'=4,'lon_0'=8,'lon_1'=2,'lon_2'=2] {'lon_0'}, use_global_device_ids=true, to_apply=%region_5.6 | all-reduce | flops 1 | bytes 8 | tf_op jit(solution)/shard_map/psum | solution.py:66
  256.0 5.9 %psum.38 = f32[]{:T(128)} all-reduce(f32[]{:T(128)} %psum.37), channel_id=1, replica_groups=mesh['lat_0'=2,'lat_1'=4,'lon_0'=8,'lon_1'=2,'lon_2'=2] {'lon_1'}, use_global_device_ids=true, to_apply=%region_6.7 | all-reduce | flops 1 | bytes 8 | tf_op jit(solution)/shard_map/psum | solution.py:66
  261.9 11.5 %psum.39 = f32[]{:T(128)} all-reduce(f32[]{:T(128)} %psum.38), channel_id=1, replica_groups=mesh['lat_0'=2,'lat_1'=4,'lon_0'=8,'lon_1'=2,'lon_2'=2] {'lon_2'}, use_global_device_ids=true, to_apply=%region_7.8 | all-reduce | flops 1 | bytes 8 | tf_op jit(solution)/shard_map/psum | solution.py:66
  276.1 23.0 %all_to_all.21 = bf16[32,2,9,512]{3,1,2,0:T(2,128)(2,1)S(1)} all-to-all(bf16[32,2,9,512]{3,1,2,0:T(2,128)(2,1)S(1)} %broadcast_in_dim.24), channel_id=1, replica_groups=mesh['lat_0'=2,'lat_1'=4,'lon_0'=8,'lon_1'=2,'lon_2'=2] {'lon_0','lon_1'..., dimensions={0} | all-to-all | bytes 1179648 | tf_op jit(solution)/shard_map/all_to_all | solution.py:40
  301.0 23.9 %all_to_all.22 = bf16[32,2,9,512]{3,1,2,0:T(2,128)(2,1)S(1)} all-to-all(bf16[32,2,9,512]{3,1,2,0:T(2,128)(2,1)S(1)} %broadcast_in_dim.25), channel_id=1, replica_groups=mesh['lat_0'=2,'lat_1'=4,'lon_0'=8,'lon_1'=2,'lon_2'=2] {'lon_0','lon_1'..., dimensions={0} | all-to-all | bytes 1179648 | tf_op jit(solution)/shard_map/all_to_all | solution.py:40
  325.6 2.8 stack.43
  328.3 4.8 %all-to-all-start.3 = ((bf16[8,64,9,512]{3,1,2,0:T(8,128)(2,1)}), bf16[8,64,9,512]{3,1,2,0:T(8,128)(2,1)}, u32[]{:S(2)}, u32[]{:S(2)}) async-start(bf16[8,64,9,512]{3,1,2,0:T(8,128)(2,1)} %stack.43), calls=%async_computation.4 | async-start | bytes 9437184 | tf_op jit(solution)/shard_map/all_to_all | solution.py:162
  333.1 6.3 %fusion.87 = (bf16[4,4,90,512]{3,2,1,0:T(8,128)(2,1)}, bf16[4,4,90,512]{3,2,1,0:T(8,128)(2,1)}, bf16[4,4,90,512]{3,2,1,0:T(8,128)(2,1)}, bf16[4,4,90,512]{3,2,1,...) fusion(bf16[4,6,92,512]{3,2,1,0:T(8,128)(2,1)S(1)} %get-tuple-e, ...), kind=kLoop, calls=%fused_computation.81 | loop fusion | bytes 26542080 | tf_op jit(solution)/shard_map/slice | solution.py:86
  341.1 2.4 reshape.79
  344.9 2.6 reshape.81
  347.5 2.5 reshape.82
  351.3 2.6 reshape.84
  353.8 2.5 reshape.85
  357.6 64.2 %all-to-all-done.3 = bf16[8,64,9,512]{3,1,2,0:T(8,128)(2,1)} async-done(((bf16[8,64,9,512]{3,1,2,0:T(8,128)(2,1)}), bf16[8,64,9,512]{3,1,2,0:T(8,128)(2,1)}, u32[]{:S(2)}, u32[]{:S(2)}) %all-to-all-start.3) | async-done | bytes 4718624 | tf_op jit(solution)/shard_map/all_to_all | solution.py:162
  421.8 5.1 %copy.80 = bf16[8,64,9,512]{3,1,0,2:T(8,128)(2,1)} copy(bf16[8,64,9,512]{3,1,2,0:T(8,128)(2,1)} %all-to-all-done.3) | data formatting | bytes 9437184 | tf_op jit(solution)/shard_map/all_to_all | solution.py:162
  427.0 2.2 fusion.73
  441.0 2.3 copy.81
  (89 shorter events, 50.2 us)
Async XLA Ops:
  7.2 9.4 %copy-start.3 = (bf16[4,4,90,512]{3,1,2,0:T(4,128)(2,1)S(1)}, bf16[4,4,90,512]{3,1,2,0:T(4,128)(2,1)}, u32[]{:S(2)}) copy-start(bf16[4,4,90,512]{3,1,2,0:T(4,128)(2,1)} %param.5) | copy-start | bytes 4423684
  7.2 177.9 %reduce-scatter.2.cloned.1.call-start = ((), (), s32[]{:S(2)}) async-start(), calls=%async_computation.6 | async-start | bytes 10616832 | tf_op jit(solution)/shard_map/reduce_scatter | solution.py:141
  11.2 11.7 %collective-permute-start = (bf16[4,1,90,512]{3,2,1,0:T(8,128)(2,1)}, bf16[4,1,90,512]{3,2,1,0:T(8,128)(2,1)}, u32[]{:S(2)}, u32[]{:S(2)}) collective-permute-start(bf16[4,1,90,512]{3,2,1,0:T(8,128)(2,1)} %copy.111), channel_id=1, source_target_pairs={{0,32},{32,64},{64,96},{96,128},{128,160},{160,192},{192,224},{224... | collective-permute-start | bytes 1105928 | tf_op jit(solution)/shard_map/ppermute | solution.py:30
  14.2 9.8 %copy-start.4 = (bf16[4,4,90,512]{3,1,2,0:T(4,128)(2,1)S(1)}, bf16[4,4,90,512]{3,1,2,0:T(4,128)(2,1)}, u32[]{:S(2)}) copy-start(bf16[4,4,90,512]{3,1,2,0:T(4,128)(2,1)} %param.6) | copy-start | bytes 4423684
  14.2 10.1 %collective-permute-start.1 = (bf16[4,1,90,512]{3,2,1,0:T(8,128)(2,1)}, bf16[4,1,90,512]{3,2,1,0:T(8,128)(2,1)}, u32[]{:S(2)}, u32[]{:S(2)}) collective-permute-start(bf16[4,1,90,512]{3,2,1,0:T(8,128)(2,1)} %copy.112), channel_id=1, source_target_pairs={{32,0},{64,32},{96,64},{128,96},{160,128},{192,160},{224,192},{0,2... | collective-permute-start | bytes 1105928 | tf_op jit(solution)/shard_map/ppermute | solution.py:33
  18.4 14.0 %collective-permute-start.4 = (bf16[4,1,90,512]{3,2,1,0:T(8,128)(2,1)}, bf16[4,1,90,512]{3,2,1,0:T(8,128)(2,1)}, u32[]{:S(2)}, u32[]{:S(2)}) collective-permute-start(bf16[4,1,90,512]{3,2,1,0:T(8,128)(2,1)} %copy.113), channel_id=1, source_target_pairs={{0,32},{32,64},{64,96},{96,128},{128,160},{160,192},{192,224},{224... | collective-permute-start | bytes 1105928 | tf_op jit(solution)/shard_map/ppermute | solution.py:30
  18.4 15.3 %collective-permute-start.5 = (bf16[4,1,90,512]{3,2,1,0:T(8,128)(2,1)S(1)}, bf16[4,1,90,512]{3,2,1,0:T(8,128)(2,1)}, u32[]{:S(2)}, u32[]{:S(2)}) collective-permute-start(bf16[4,1,90,512]{3,2,1,0:T(8,128)(2,1)S(1)} %copy.114), channel_id=1, source_target_pairs={{32,0},{64,32},{96,64},{128,96},{160,128},{192,160},{224,192},{0,2... | collective-permute-start | bytes 1105928 | tf_op jit(solution)/shard_map/ppermute | solution.py:33
  25.4 25.3 %collective-permute-start.2 = (bf16[4,6,1,512]{3,2,1,0:T(2,128)(2,1)S(1)}, bf16[4,6,1,512]{3,2,1,0:T(2,128)(2,1)S(1)}, u32[]{:S(2)}, u32[]{:S(2)}) collective-permute-start(bf16[4,6,1,512]{3,2,1,0:T(2,128)(2,1)S(1)} %get-tuple-element.46), channel_id=1, source_target_pairs={{0,1},{1,2},{2,3},{3,4},{4,5},{5,6},{6,7},{7,8},{8,9},{9,10},{10,1... | collective-permute-start | bytes 73736 | tf_op jit(solution)/shard_map/ppermute | solution.py:30
  32.3 18.4 %collective-permute-start.3 = (bf16[4,6,1,512]{3,2,1,0:T(2,128)(2,1)S(1)}, bf16[4,6,1,512]{3,2,1,0:T(2,128)(2,1)S(1)}, u32[]{:S(2)}, u32[]{:S(2)}) collective-permute-start(bf16[4,6,1,512]{3,2,1,0:T(2,128)(2,1)S(1)} %get-tuple-element.47), channel_id=1, source_target_pairs={{1,0},{2,1},{3,2},{4,3},{5,4},{6,5},{7,6},{8,7},{9,8},{10,9},{11,1... | collective-permute-start | bytes 73736 | tf_op jit(solution)/shard_map/ppermute | solution.py:33
  34.8 16.0 %collective-permute-start.6 = (bf16[4,6,1,512]{3,2,1,0:T(2,128)(2,1)S(1)}, bf16[4,6,1,512]{3,2,1,0:T(2,128)(2,1)S(1)}, u32[]{:S(2)}, u32[]{:S(2)}) collective-permute-start(bf16[4,6,1,512]{3,2,1,0:T(2,128)(2,1)S(1)} %get-tuple-element.35), channel_id=1, source_target_pairs={{0,1},{1,2},{2,3},{3,4},{4,5},{5,6},{6,7},{7,8},{8,9},{9,10},{10,1... | collective-permute-start | bytes 73736 | tf_op jit(solution)/shard_map/ppermute | solution.py:30
  39.6 16.1 %collective-permute-start.7 = (bf16[4,6,1,512]{3,2,1,0:T(2,128)(2,1)S(1)}, bf16[4,6,1,512]{3,2,1,0:T(2,128)(2,1)S(1)}, u32[]{:S(2)}, u32[]{:S(2)}) collective-permute-start(bf16[4,6,1,512]{3,2,1,0:T(2,128)(2,1)S(1)} %get-tuple-element.36), channel_id=1, source_target_pairs={{1,0},{2,1},{3,2},{4,3},{5,4},{6,5},{7,6},{8,7},{9,8},{10,9},{11,1... | collective-permute-start | bytes 73736 | tf_op jit(solution)/shard_map/ppermute | solution.py:33
  50.8 7.7 %copy-start.5 = (bf16[4,4,90,512]{3,1,2,0:T(4,128)(2,1)S(1)}, bf16[4,4,90,512]{3,1,2,0:T(4,128)(2,1)}, u32[]{:S(2)}) copy-start(bf16[4,4,90,512]{3,1,2,0:T(4,128)(2,1)} %param.6) | copy-start | bytes 4423684
  76.7 350.2 %all-gather.2.cloned.1.call-start = ((), (), s32[]{:S(2)}) async-start(), calls=%async_computation.5 | async-start | bytes 5308416 | tf_op jit(solution)/shard_map/all_gather | solution.py:138
  328.3 93.5 %all-to-all-start.3 = ((bf16[8,64,9,512]{3,1,2,0:T(8,128)(2,1)}), bf16[8,64,9,512]{3,1,2,0:T(8,128)(2,1)}, u32[]{:S(2)}, u32[]{:S(2)}) async-start(bf16[8,64,9,512]{3,1,2,0:T(8,128)(2,1)} %stack.43), calls=%async_computation.4 | async-start | bytes 9437184 | tf_op jit(solution)/shard_map/all_to_all | solution.py:162
  339.4 4.2 copy-start.2
  344.9 5.1 %copy-start.1 = (bf16[4,4,90,512]{3,2,1,0:T(8,128)(2,1)S(1)}, bf16[4,4,90,512]{3,2,1,0:T(8,128)(2,1)}, u32[]{:S(2)}) copy-start(bf16[4,4,90,512]{3,2,1,0:T(8,128)(2,1)} %get-tuple-element.40) | copy-start | bytes 4423684
  351.3 5.0 %copy-start = (bf16[4,4,90,512]{3,2,1,0:T(8,128)(2,1)S(1)}, bf16[4,4,90,512]{3,2,1,0:T(8,128)(2,1)}, u32[]{:S(2)}) copy-start(bf16[4,4,90,512]{3,2,1,0:T(8,128)(2,1)} %get-tuple-element.37) | copy-start | bytes 4423684
  427.0 2.2 copy-start.13
  427.0 2.9 copy-start.14
  429.9 1.4 copy-start.12
  431.3 1.4 copy-start.11
  432.6 1.4 copy-start.10
  434.0 1.4 copy-start.9
  435.4 1.4 copy-start.8
  436.8 1.4 copy-start.7
  438.1 1.4 copy-start.6
Sparse Core Ops, SparseCore 0:
  76.9 108.1 reduce-scatter.1
  300.8 102.7 all-gather.1
